TPU v7x, 32 devices: a whole 2x2x4 slice. The times are simulated.
32 devices in a mesh: gx: 8 (over z, y), gy: 4 (over x, core).
Axes of the slice: x: 2, y: 2, z: 4, core: 2. Of those that a mesh axis runs over, the one named last changes fastest.
Arguments:
- rhs: bfloat16 [512, 32768], P(None, ('gy', 'gx')), may hold values from -6 to 6
- leaf_inverse: bfloat16 [32, 1024, 1024], P(('gy', 'gx')), may hold values from -0.1875 to 0.1875
- up_basis: bfloat16 [5, 128, 32768], P(None, None, ('gy', 'gx')), may hold values from -0.25 to 0.25
- projection: bfloat16 [5, 256, 32768], P(None, None, ('gy', 'gx')), may hold values from -0.13258252 to 0.13258252, as said below
Outputs:
- solution: float32 [512, 32768], P(None, ('gy', 'gx'))
Inputs may be any that keep to these rules, and one draw needn't show every extreme that they name: `projection`: rows of level h (counted from 1) have entries of order (2^h * 1024)^(-1/2).
All inputs are finite; a program needn't handle non-finite values.
Results may differ from a plain program's by a relative error of at most 0.0095.
Values sent between devices are 32-bit elements; how exact they have to be, the bound alone decides.
A program may use at most 64 MiB of HBM per device.

v0:
```python
import jax
import jax.numpy as jnp
from jax import lax
from jax.sharding import PartitionSpec as P

RANK = 128


def partner(value, axis, stride):
    mask = 2**stride
    pairs = [(source, source ^ mask) for source in range(lax.axis_size(axis))]
    return lax.ppermute(value, axis, pairs)


def own_half(partial_value, child_bit):
    return lax.dynamic_slice_in_dim(partial_value, child_bit * RANK, RANK, 1)


def node_sum(partial_value, height, bits_x, child_bit):
    mine = own_half(partial_value, child_bit)
    other = own_half(partial_value, 1 - child_bit)
    if height <= bits_x:
        for bit_pos in range(height):
            partial_value = partial_value + partner(partial_value, "gx", bit_pos)
        return own_half(partial_value, child_bit)
    total = mine + partner(other, "gy", height - 1 - bits_x)
    for bit_pos in range(bits_x):
        total = total + partner(total, "gx", bit_pos)
    for bit_pos in range(height - 1 - bits_x):
        total = total + partner(total, "gy", bit_pos)
    return total


def shards(rhs, leaf_inverse, up_basis, projection):
    size_x = lax.axis_size("gx")
    bits_x = size_x.bit_length() - 1
    bits_y = lax.axis_size("gy").bit_length() - 1
    leaf_pos = lax.axis_index("gy") * size_x + lax.axis_index("gx")
    state = jnp.dot(rhs, leaf_inverse[0], preferred_element_type=jnp.float32)
    for height in range(1, bits_x + bits_y + 1):
        rounded = state.astype(jnp.bfloat16)
        partial_value = lax.dot_general(
            rounded,
            projection[height - 1],
            (((1,), (1,)), ((), ())),
            preferred_element_type=jnp.float32,
        )
        child_bit = leaf_pos >> height - 1 & 1
        node_total = node_sum(partial_value, height, bits_x, child_bit)
        coefficient = node_total.astype(jnp.bfloat16)
        state = state - jnp.dot(
            coefficient, up_basis[height - 1], preferred_element_type=jnp.float32
        )
    return state


def solution(mesh):
    return jax.shard_map(
        shards,
        mesh=mesh,
        in_specs=(
            P(None, ("gy", "gx")),
            P(("gy", "gx"), None, None),
            P(None, None, ("gy", "gx")),
            P(None, None, ("gy", "gx")),
        ),
        out_specs=P(None, ("gy", "gx")),
        check_vma=False,
    )
```

profile of v0, /device:TPU:0, one launch (start us, length us, event | category | flops | bytes accessed | tf_op | source)
XLA Modules:
  0.0 182.8 jit_solution(2986032395950507599)
XLA Ops:
  0.0 1.6 copy-done
  1.6 2.5 %fusion = f32[512,1024]{1,0:T(8,128)S(1)} fusion(bf16[512,1024]{1,0:T(8,128)(2,1)} %param.4, bf16[1,1024,1024]{2,1,0:T(8,128)(2,1)S(1)} %copy-done), kind=kOutput, calls=%fused_computation | convolution fusion | flops 1073741824 | bytes 5242880 | tf_op jit(solution)/shard_map/dot_general | solution.py:39
  5.4 2.4 %fusion.10 = f32[512,256]{1,0:T(8,128)} fusion(f32[512,1024]{1,0:T(8,128)S(1)} %fusion, bf16[5,256,1024]{2,1,0:T(8,128)(2,1)} %param.7), kind=kOutput, calls=%fused_computation.15 | convolution fusion | flops 268959744 | bytes 3145728 | tf_op jit(solution)/shard_map/dot_general | solution.py:42
  7.8 3.0 %collective-permute-start = (f32[512,256]{1,0:T(8,128)}, f32[512,256]{1,0:T(8,128)}, u32[]{:S(2)}, u32[]{:S(2)}) collective-permute-start(f32[512,256]{1,0:T(8,128)} %fusion.10), channel_id=1, source_target_pairs={{0,4},{4,0},{8,12},{12,8},{16,20},{20,16},{24,28},{28,24},{1,5},{5... | collective-permute-start | bytes 1572872 | tf_op jit(solution)/shard_map/ppermute | solution.py:12
  10.8 12.2 %collective-permute-done = f32[512,256]{1,0:T(8,128)} collective-permute-done((f32[512,256]{1,0:T(8,128)}, f32[512,256]{1,0:T(8,128)}, u32[]{:S(2)}, u32[]{:S(2)}) %collective-permute-start) | collective-permute-done | bytes 524320 | tf_op jit(solution)/shard_map/ppermute | solution.py:12
  23.1 2.2 %convolution_subtract_fusion.4 = f32[512,1024]{1,0:T(8,128)S(1)} fusion(f32[512,1024]{1,0:T(8,128)} %copy-done.6, bf16[5,128,1024]{2,1,0:T(8,128)(2,1)S(1)} %copy-done.7, f32[512,256]{1,0:T(8,128)} %collective-permute-done, s32[]{:T(128)S(6)} %select_n.21, f32[512,256]{1,0:T(8,128)} %fusion.10), kind=kOutput, calls=%fused_computation.6 | convolution fusion | flops 134873088 | bytes 4980740 | tf_op jit(solution)/shard_map/dot_general | solution.py:51
  25.3 1.9 %fusion.8 = f32[512,256]{1,0:T(8,128)S(1)} fusion(f32[512,1024]{1,0:T(8,128)S(1)} %convolution_subtract_fusion.4, bf16[5,256,1024]{2,1,0:T(8,128)(2,1)} %param.7), kind=kOutput, calls=%fused_computation.13 | convolution fusion | flops 268959744 | bytes 3145728 | tf_op jit(solution)/shard_map/dot_general | solution.py:42
  27.2 1.8 collective-permute-start.1
  29.0 11.3 %collective-permute-done.1 = f32[512,256]{1,0:T(8,128)S(1)} collective-permute-done((f32[512,256]{1,0:T(8,128)S(1)}, f32[512,256]{1,0:T(8,128)S(1)}, u32[]{:S(2)}, u32[]{:S(2)}) %collective-permute-start.1) | collective-permute-done | bytes 524320 | tf_op jit(solution)/shard_map/ppermute | solution.py:12
  41.2 1.5 collective-permute-start.2
  42.7 11.0 %collective-permute-done.2 = f32[512,256]{1,0:T(8,128)} collective-permute-done((f32[512,256]{1,0:T(8,128)}, f32[512,256]{1,0:T(8,128)}, u32[]{:S(2)}, u32[]{:S(2)}) %collective-permute-start.2) | collective-permute-done | bytes 524320 | tf_op jit(solution)/shard_map/ppermute | solution.py:12
  53.8 2.2 %convolution_subtract_fusion.3 = f32[512,1024]{1,0:T(8,128)S(1)} fusion(f32[512,1024]{1,0:T(8,128)} %copy-done.5, bf16[5,128,1024]{2,1,0:T(8,128)(2,1)S(1)} %copy-done.7, f32[512,256]{1,0:T(8,128)} %collective-permute-done.2, s32[]{:T(128)S(6)} %select_n.22, f32[512,256]{1,0:T(8,128)} %add.72), kind=kOutput, calls=%fused_computation.5 | convolution fusion | flops 134873088 | bytes 4980740 | tf_op jit(solution)/shard_map/dot_general | solution.py:51
  56.0 1.9 %fusion.6 = f32[512,256]{1,0:T(8,128)S(1)} fusion(f32[512,1024]{1,0:T(8,128)S(1)} %convolution_subtract_fusion.3, bf16[5,256,1024]{2,1,0:T(8,128)(2,1)} %param.7), kind=kOutput, calls=%fused_computation.11 | convolution fusion | flops 268959744 | bytes 3145728 | tf_op jit(solution)/shard_map/dot_general | solution.py:42
  59.1 10.2 %collective-permute-done.3 = f32[512,256]{1,0:T(8,128)S(1)} collective-permute-done((f32[512,256]{1,0:T(8,128)S(1)}, f32[512,256]{1,0:T(8,128)S(1)}, u32[]{:S(2)}, u32[]{:S(2)}) %collective-permute-start.3) | collective-permute-done | bytes 524320 | tf_op jit(solution)/shard_map/ppermute | solution.py:12
  70.4 9.6 %collective-permute-done.4 = f32[512,256]{1,0:T(8,128)S(1)} collective-permute-done((f32[512,256]{1,0:T(8,128)S(1)}, f32[512,256]{1,0:T(8,128)S(1)}, u32[]{:S(2)}, u32[]{:S(2)}) %collective-permute-start.4) | collective-permute-done | bytes 524320 | tf_op jit(solution)/shard_map/ppermute | solution.py:12
  80.9 2.5 %collective-permute-start.5 = (f32[512,256]{1,0:T(8,128)}, f32[512,256]{1,0:T(8,128)}, u32[]{:S(2)}, u32[]{:S(2)}) collective-permute-start(f32[512,256]{1,0:T(8,128)} %add.76), channel_id=1, source_target_pairs={{0,16},{4,20},{8,24},{12,28},{16,0},{20,4},{24,8},{28,12},{1,17},{... | collective-permute-start | bytes 1572872 | tf_op jit(solution)/shard_map/ppermute | solution.py:12
  83.4 19.5 %collective-permute-done.5 = f32[512,256]{1,0:T(8,128)} collective-permute-done((f32[512,256]{1,0:T(8,128)}, f32[512,256]{1,0:T(8,128)}, u32[]{:S(2)}, u32[]{:S(2)}) %collective-permute-start.5) | collective-permute-done | bytes 524320 | tf_op jit(solution)/shard_map/ppermute | solution.py:12
  102.9 2.2 %convolution_subtract_fusion.2 = f32[512,1024]{1,0:T(8,128)S(1)} fusion(f32[512,1024]{1,0:T(8,128)} %copy-done.4, bf16[5,128,1024]{2,1,0:T(8,128)(2,1)S(1)} %copy-done.7, f32[512,256]{1,0:T(8,128)} %collective-permute-done.5, s32[]{:T(128)S(6)} %select_n.23, f32[512,256]{1,0:T(8,128)} %add.76), kind=kOutput, calls=%fused_computation.4 | convolution fusion | flops 134873088 | bytes 4980740 | tf_op jit(solution)/shard_map/dot_general | solution.py:51
  105.1 1.3 copy-done.1
  106.4 1.5 fusion.4
  108.1 1.5 collective-permute-done.6
  110.1 8.0 %collective-permute-done.7 = f32[512,128]{1,0:T(8,128)S(1)} collective-permute-done((f32[512,128]{1,0:T(8,128)S(1)}, f32[512,128]{1,0:T(8,128)S(1)}, u32[]{:S(2)}, u32[]{:S(2)}) %collective-permute-start.7) | collective-permute-done | bytes 262176 | tf_op jit(solution)/shard_map/ppermute | solution.py:12
  118.2 7.5 %collective-permute-done.8 = f32[512,128]{1,0:T(8,128)S(1)} collective-permute-done((f32[512,128]{1,0:T(8,128)S(1)}, f32[512,128]{1,0:T(8,128)S(1)}, u32[]{:S(2)}, u32[]{:S(2)}) %collective-permute-start.8) | collective-permute-done | bytes 262176 | tf_op jit(solution)/shard_map/ppermute | solution.py:12
  126.9 12.0 %collective-permute-done.9 = f32[512,128]{1,0:T(8,128)S(1)} collective-permute-done((f32[512,128]{1,0:T(8,128)S(1)}, f32[512,128]{1,0:T(8,128)S(1)}, u32[]{:S(2)}, u32[]{:S(2)}) %collective-permute-start.9) | collective-permute-done | bytes 262176 | tf_op jit(solution)/shard_map/ppermute | solution.py:12
  138.9 2.1 %convolution_subtract_fusion.1 = f32[512,1024]{1,0:T(8,128)S(1)} fusion(f32[512,1024]{1,0:T(8,128)} %copy-done.1, bf16[5,128,1024]{2,1,0:T(8,128)(2,1)} %param.6, f32[512,128]{1,0:T(8,128)S(1)} %add.83, f32[512,128]{1,0:T(8,128)S(1)} %collective-permute-done.9), kind=kOutput, calls=%fused_computation.3 | convolution fusion | flops 134873088 | bytes 4980736 | tf_op jit(solution)/shard_map/dot_general | solution.py:51
  142.3 1.5 fusion.2
  144.3 7.9 %collective-permute-done.10 = f32[512,128]{1,0:T(8,128)S(1)} collective-permute-done((f32[512,128]{1,0:T(8,128)S(1)}, f32[512,128]{1,0:T(8,128)S(1)}, u32[]{:S(2)}, u32[]{:S(2)}) %collective-permute-start.10) | collective-permute-done | bytes 262176 | tf_op jit(solution)/shard_map/ppermute | solution.py:12
  152.3 7.4 %collective-permute-done.11 = f32[512,128]{1,0:T(8,128)S(1)} collective-permute-done((f32[512,128]{1,0:T(8,128)S(1)}, f32[512,128]{1,0:T(8,128)S(1)}, u32[]{:S(2)}, u32[]{:S(2)}) %collective-permute-start.11) | collective-permute-done | bytes 262176 | tf_op jit(solution)/shard_map/ppermute | solution.py:12
  159.8 6.5 %collective-permute-done.12 = f32[512,128]{1,0:T(8,128)S(1)} collective-permute-done((f32[512,128]{1,0:T(8,128)S(1)}, f32[512,128]{1,0:T(8,128)S(1)}, u32[]{:S(2)}, u32[]{:S(2)}) %collective-permute-start.12) | collective-permute-done | bytes 262176 | tf_op jit(solution)/shard_map/ppermute | solution.py:12
  167.5 11.0 %collective-permute-done.13 = f32[512,128]{1,0:T(8,128)S(1)} collective-permute-done((f32[512,128]{1,0:T(8,128)S(1)}, f32[512,128]{1,0:T(8,128)S(1)}, u32[]{:S(2)}, u32[]{:S(2)}) %collective-permute-start.13) | collective-permute-done | bytes 262176 | tf_op jit(solution)/shard_map/ppermute | solution.py:12
  178.6 1.5 collective-permute-done.14
  180.2 2.7 %convolution_subtract_fusion = f32[512,1024]{1,0:T(8,128)} fusion(f32[512,1024]{1,0:T(8,128)S(1)} %copy-done.3, bf16[5,128,1024]{2,1,0:T(8,128)(2,1)} %param.6, f32[512,128]{1,0:T(8,128)S(1)} %add.90, f32[512,128]{1,0:T(8,128)S(1)} %collective-permute-done.14), kind=kOutput, calls=%fused_computation.2 | convolution fusion | flops 134873088 | bytes 4980736 | tf_op jit(solution)/shard_map/dot_general | solution.py:51
  (37 shorter events, 10.7 us)
Async XLA Ops:
  0.0 1.6 copy-start
  4.1 1.3 copy-start.6
  5.4 17.7 %copy-start.7 = (bf16[5,128,1024]{2,1,0:T(8,128)(2,1)S(1)}, bf16[5,128,1024]{2,1,0:T(8,128)(2,1)}, u32[]{:S(2)}) copy-start(bf16[5,128,1024]{2,1,0:T(8,128)(2,1)} %param.6) | copy-start | bytes 3932164
  7.8 15.2 %collective-permute-start = (f32[512,256]{1,0:T(8,128)}, f32[512,256]{1,0:T(8,128)}, u32[]{:S(2)}, u32[]{:S(2)}) collective-permute-start(f32[512,256]{1,0:T(8,128)} %fusion.10), channel_id=1, source_target_pairs={{0,4},{4,0},{8,12},{12,8},{16,20},{20,16},{24,28},{28,24},{1,5},{5... | collective-permute-start | bytes 1572872 | tf_op jit(solution)/shard_map/ppermute | solution.py:12
  25.3 16.0 %copy-start.5 = (f32[512,1024]{1,0:T(8,128)}, f32[512,1024]{1,0:T(8,128)S(1)}, u32[]{:S(2)}) copy-start(f32[512,1024]{1,0:T(8,128)S(1)} %convolution_subtract_fusion.4) | copy-start | bytes 6291460
  27.2 13.2 %collective-permute-start.1 = (f32[512,256]{1,0:T(8,128)S(1)}, f32[512,256]{1,0:T(8,128)S(1)}, u32[]{:S(2)}, u32[]{:S(2)}) collective-permute-start(f32[512,256]{1,0:T(8,128)S(1)} %fusion.8), channel_id=1, source_target_pairs={{0,4},{4,0},{8,12},{12,8},{16,20},{20,16},{24,28},{28,24},{1,5},{5... | collective-permute-start | bytes 1572872 | tf_op jit(solution)/shard_map/ppermute | solution.py:12
  41.2 12.6 %collective-permute-start.2 = (f32[512,256]{1,0:T(8,128)}, f32[512,256]{1,0:T(8,128)}, u32[]{:S(2)}, u32[]{:S(2)}) collective-permute-start(f32[512,256]{1,0:T(8,128)} %add.72), channel_id=1, source_target_pairs={{0,8},{4,12},{8,0},{12,4},{16,24},{20,28},{24,16},{28,20},{1,9},{5... | collective-permute-start | bytes 1572872 | tf_op jit(solution)/shard_map/ppermute | solution.py:12
  56.0 13.4 %copy-start.4 = (f32[512,1024]{1,0:T(8,128)}, f32[512,1024]{1,0:T(8,128)S(1)}, u32[]{:S(2)}) copy-start(f32[512,1024]{1,0:T(8,128)S(1)} %convolution_subtract_fusion.3) | copy-start | bytes 6291460
  57.9 11.4 %collective-permute-start.3 = (f32[512,256]{1,0:T(8,128)S(1)}, f32[512,256]{1,0:T(8,128)S(1)}, u32[]{:S(2)}, u32[]{:S(2)}) collective-permute-start(f32[512,256]{1,0:T(8,128)S(1)} %fusion.6), channel_id=1, source_target_pairs={{0,4},{4,0},{8,12},{12,8},{16,20},{20,16},{24,28},{28,24},{1,5},{5... | collective-permute-start | bytes 1572872 | tf_op jit(solution)/shard_map/ppermute | solution.py:12
  69.4 10.6 %collective-permute-start.4 = (f32[512,256]{1,0:T(8,128)S(1)}, f32[512,256]{1,0:T(8,128)S(1)}, u32[]{:S(2)}, u32[]{:S(2)}) collective-permute-start(f32[512,256]{1,0:T(8,128)S(1)} %add.75), channel_id=1, source_target_pairs={{0,8},{4,12},{8,0},{12,4},{16,24},{20,28},{24,16},{28,20},{1,9},{5... | collective-permute-start | bytes 1572872 | tf_op jit(solution)/shard_map/ppermute | solution.py:12
  80.9 22.0 %collective-permute-start.5 = (f32[512,256]{1,0:T(8,128)}, f32[512,256]{1,0:T(8,128)}, u32[]{:S(2)}, u32[]{:S(2)}) collective-permute-start(f32[512,256]{1,0:T(8,128)} %add.76), channel_id=1, source_target_pairs={{0,16},{4,20},{8,24},{12,28},{16,0},{20,4},{24,8},{28,12},{1,17},{... | collective-permute-start | bytes 1572872 | tf_op jit(solution)/shard_map/ppermute | solution.py:12
  105.1 1.3 copy-start.1
  108.0 1.6 collective-permute-start.6
  109.6 8.4 %collective-permute-start.7 = (f32[512,128]{1,0:T(8,128)S(1)}, f32[512,128]{1,0:T(8,128)S(1)}, u32[]{:S(2)}, u32[]{:S(2)}) collective-permute-start(f32[512,128]{1,0:T(8,128)S(1)} %dynamic-slice_add_fusion.4), channel_id=1, source_target_pairs={{0,4},{4,0},{8,12},{12,8},{16,20},{20,16},{24,28},{28,24},{1,5},{5... | collective-permute-start | bytes 786440 | tf_op jit(solution)/shard_map/ppermute | solution.py:12
  118.1 7.6 %collective-permute-start.8 = (f32[512,128]{1,0:T(8,128)S(1)}, f32[512,128]{1,0:T(8,128)S(1)}, u32[]{:S(2)}, u32[]{:S(2)}) collective-permute-start(f32[512,128]{1,0:T(8,128)S(1)} %add.82), channel_id=1, source_target_pairs={{0,8},{4,12},{8,0},{12,4},{16,24},{20,28},{24,16},{28,20},{1,9},{5... | collective-permute-start | bytes 786440 | tf_op jit(solution)/shard_map/ppermute | solution.py:12
  125.7 13.2 %collective-permute-start.9 = (f32[512,128]{1,0:T(8,128)S(1)}, f32[512,128]{1,0:T(8,128)S(1)}, u32[]{:S(2)}, u32[]{:S(2)}) collective-permute-start(f32[512,128]{1,0:T(8,128)S(1)} %add.83), channel_id=1, source_target_pairs={{0,16},{4,20},{8,24},{12,28},{16,0},{20,4},{24,8},{28,12},{1,17},{... | collective-permute-start | bytes 786440 | tf_op jit(solution)/shard_map/ppermute | solution.py:12
  141.0 1.3 copy-start.2
  143.9 8.3 %collective-permute-start.10 = (f32[512,128]{1,0:T(8,128)S(1)}, f32[512,128]{1,0:T(8,128)S(1)}, u32[]{:S(2)}, u32[]{:S(2)}) collective-permute-start(f32[512,128]{1,0:T(8,128)S(1)} %constant_dynamic-slice_fusion), channel_id=1, source_target_pairs={{0,2},{1,3},{2,0},{3,1},{4,6},{5,7},{6,4},{7,5},{8,10},{9,11},{10,... | collective-permute-start | bytes 786440 | tf_op jit(solution)/shard_map/ppermute | solution.py:12
  144.3 35.8 %copy-start.3 = (f32[512,1024]{1,0:T(8,128)S(1)}, f32[512,1024]{1,0:T(8,128)}, u32[]{:S(2)}) copy-start(f32[512,1024]{1,0:T(8,128)} %copy-done.2) | copy-start | bytes 6291460
  152.2 7.4 %collective-permute-start.11 = (f32[512,128]{1,0:T(8,128)S(1)}, f32[512,128]{1,0:T(8,128)S(1)}, u32[]{:S(2)}, u32[]{:S(2)}) collective-permute-start(f32[512,128]{1,0:T(8,128)S(1)} %dynamic-slice_add_fusion.3), channel_id=1, source_target_pairs={{0,4},{4,0},{8,12},{12,8},{16,20},{20,16},{24,28},{28,24},{1,5},{5... | collective-permute-start | bytes 786440 | tf_op jit(solution)/shard_map/ppermute | solution.py:12
  159.7 6.6 %collective-permute-start.12 = (f32[512,128]{1,0:T(8,128)S(1)}, f32[512,128]{1,0:T(8,128)S(1)}, u32[]{:S(2)}, u32[]{:S(2)}) collective-permute-start(f32[512,128]{1,0:T(8,128)S(1)} %add.88), channel_id=1, source_target_pairs={{0,8},{4,12},{8,0},{12,4},{16,24},{20,28},{24,16},{28,20},{1,9},{5... | collective-permute-start | bytes 786440 | tf_op jit(solution)/shard_map/ppermute | solution.py:12
  166.3 12.2 %collective-permute-start.13 = (f32[512,128]{1,0:T(8,128)S(1)}, f32[512,128]{1,0:T(8,128)S(1)}, u32[]{:S(2)}, u32[]{:S(2)}) collective-permute-start(f32[512,128]{1,0:T(8,128)S(1)} %add.89), channel_id=1, source_target_pairs={{0,16},{4,20},{8,24},{12,28},{16,0},{20,4},{24,8},{28,12},{1,17},{... | collective-permute-start | bytes 786440 | tf_op jit(solution)/shard_map/ppermute | solution.py:12
  178.6 1.6 collective-permute-start.14
where the time goes:
time: 183 us
  waiting for transfers between devices  137 us (75%)
  matrix products  23.1 us (13%)
  starting transfers between devices  14.8 us (8%)
  local copies, waits for them, and re-layouts  5.61 us (3%)
  other arithmetic  2.02 us (1%)
    ppermute x15, waiting for transfers between devices, partner(): return lax.ppermute(value, axis, pairs)  137 us
    ppermute x15, starting transfers between devices, partner(): return lax.ppermute(value, axis, pairs)  14.8 us
    dot_general x5, matrix products, shards(): jnp.dot(coefficient, up_basis[height - 1], preferred_element_type=jnp.flo...  11.4 us
    dot_general x5, matrix products, shards(): lax.dot_general(rounded, projection[height - 1], (((1,), (1,)), ((), ()))...  9.27 us
    unnamed x16, local copies, waits for them, and re-layouts  5.55 us
  transfers between devices with their start and end apart: 15, of which 15 were waited for; matrix products, arithmetic and copies ran while one was open for 0% of the time, Pallas kernels for 0%

commit v1 on v0

v1 whole, which is shorter than its diff:
```python
import functools

import jax
import jax.numpy as jnp
from jax import lax
from jax.experimental import pallas as pl
from jax.experimental.pallas import tpu as pltpu
from jax.sharding import PartitionSpec as P

CHUNKS = 2
SUBLANES = 8
TILE = 256
F32 = jnp.float32
BF16 = jnp.bfloat16


def level_plan(height, bits_x, rows):
    top = height - 1
    groups = []
    low = [b for b in range(min(top, bits_x))]
    high = [b for b in range(bits_x, top)]
    if top == bits_x:
        groups.append([top])
    elif top > bits_x:
        groups.append([bits_x])
        groups.append([top] + high[1:])
    if top < bits_x and len(low) < 2:
        groups.append(low + [top])
    else:
        while low:
            groups.append(low[:2])
            low = low[2:]
        if top < bits_x:
            groups.append([top])
    phases = []
    for bits in groups:
        split = [b for b in bits if b != top]
        if rows >> len(split) < SUBLANES:
            assert top not in bits
            phases.append(("sum", bits))
        else:
            rows >>= len(split)
            phases.append(("scatter", bits))
    return phases


def masks_of(bits):
    masks = [0]
    for b in bits:
        masks += [m | 1 << b for m in masks]
    return masks[1:]


def sub_index(pos, bits):
    index = 0
    for k, b in enumerate(bits):
        index = index + ((pos >> b) & 1) * (1 << k)
    return index


def build_plan(levels, bits_x, rows, rank):
    plan, shapes, sems = [], [], 0

    def buf(*shape):
        shapes.append(shape)
        return len(shapes) - 1

    for height in range(1, levels + 1):
        top = height - 1
        n, c = rows, 2
        source = buf(c, n, rank)
        steps = []
        for kind, bits in level_plan(height, bits_x, rows):
            masks = masks_of(bits)
            split = [b for b in bits if b != top] if kind == "scatter" else []
            n >>= len(split)
            if top in bits:
                c = 1
            landing = buf(len(masks), c, n, rank)
            result = buf(c, n, rank)
            steps.append((kind, bits, split, masks, source, landing, result, n, c, sems))
            sems += len(masks)
            source = result
        for _, bits, split, *_ in reversed(list(steps)):
            if not split:
                continue
            masks = masks_of(split)
            result = buf(1, n << len(split), rank)
            steps.append(("gather", split, split, masks, source, None, result, n, 1, sems))
            sems += len(masks)
            n <<= len(split)
            source = result
        plan.append(steps)
    return plan, shapes, sems


def kernel(dims, plan, rhs_hbm, leaf_hbm, up_hbm, proj_hbm, out_hbm, *scratch):
    bits_x, bits_y, levels, chunks, rows, points, rank = dims
    rhs, leaf, up, proj, state, rounded = scratch[:6]
    in_sems, out_sems, send_sems, recv_sems = scratch[6:10]
    per_chunk = (len(scratch) - 10) // chunks
    gx, gy = lax.axis_index("gx"), lax.axis_index("gy")
    pos = gy * (1 << bits_x) + gx

    def device(mask):
        return {"gx": gx ^ (mask & ((1 << bits_x) - 1)), "gy": gy ^ (mask >> bits_x)}

    loads = [
        pltpu.make_async_copy(rhs_hbm, rhs, in_sems.at[0]),
        pltpu.make_async_copy(leaf_hbm.at[0], leaf, in_sems.at[1]),
    ]
    for level in range(levels):
        loads.append(pltpu.make_async_copy(proj_hbm.at[level], proj.at[level], in_sems.at[2 + 2 * level]))
        loads.append(pltpu.make_async_copy(up_hbm.at[level], up.at[level], in_sems.at[3 + 2 * level]))
    for load in loads:
        load.start()

    everyone = set()
    for steps in plan:
        for step in steps:
            everyone.update(step[3])
    barrier = pltpu.get_barrier_semaphore()
    for mask in sorted(everyone):
        pl.semaphore_signal(barrier, inc=1, device_id=device(mask), device_id_type=pl.DeviceIdType.MESH)
    loads[0].wait()
    loads[1].wait()

    def leaf_apply(lo):
        @pl.loop(0, points // TILE)
        def _(tile):
            cols = pl.ds(pl.multiple_of(tile * TILE, TILE), TILE)
            value = jnp.dot(rhs[lo : lo + rows, :], leaf[:, cols], preferred_element_type=F32)
            state[lo : lo + rows, cols] = value
            rounded[lo : lo + rows, cols] = value.astype(BF16)

    def update(lo, level, coefficient):
        @pl.loop(0, points // TILE)
        def _(tile):
            cols = pl.ds(pl.multiple_of(tile * TILE, TILE), TILE)
            value = state[lo : lo + rows, cols] - jnp.dot(
                coefficient, up[level, :, cols], preferred_element_type=F32
            )
            state[lo : lo + rows, cols] = value
            rounded[lo : lo + rows, cols] = value.astype(BF16)

    leaf_apply(0)
    pl.semaphore_wait(barrier, len(everyone))

    def flow(chunk):
        lo = chunk * rows
        bufs = scratch[10 + chunk * per_chunk : 10 + (chunk + 1) * per_chunk]
        if chunk:
            leaf_apply(lo)
        sends = []
        for level in range(levels):
            top = level
            if chunk == 0:
                loads[2 + 2 * level].wait()
            whole = bufs[plan[level][0][4]]
            for half in range(2):
                whole[half] = lax.dot_general(
                    rounded[lo : lo + rows, :],
                    proj[level, half * rank : (half + 1) * rank, :],
                    (((1,), (1,)), ((), ())),
                    preferred_element_type=F32,
                )
            bit = (pos >> top) & 1
            for kind, bits, split, masks, src, landing, dst, n, c, sem in plan[level]:
                copies = []
                src_ref, dst_ref = bufs[src], bufs[dst]

                def piece(who):
                    row = pl.ds(pl.multiple_of(sub_index(who, split) * n, n), n)
                    if top in bits:
                        return pl.ds((who >> top) & 1, 1), row
                    return pl.ds(0, c), row

                if kind == "gather":
                    own = pl.ds(pl.multiple_of(sub_index(pos, split) * n, n), n)
                for k, mask in enumerate(masks):
                    if kind == "gather":
                        frm, to = src_ref, dst_ref.at[:, own]
                    else:
                        frm, to = src_ref.at[piece(pos ^ mask)], bufs[landing].at[k]
                    copy = pltpu.make_async_remote_copy(
                        src_ref=frm,
                        dst_ref=to,
                        send_sem=send_sems.at[chunk, sem + k],
                        recv_sem=recv_sems.at[chunk, sem + k],
                        device_id=device(mask),
                        device_id_type=pl.DeviceIdType.MESH,
                    )
                    copy.start()
                    copies.append(copy)
                sends += copies
                if kind == "gather":
                    dst_ref[:, own] = src_ref[...]
                yield
                if kind == "gather":
                    for copy in copies:
                        copy.wait_recv()
                else:
                    for copy in copies:
                        copy.wait_recv()
                    total = src_ref[piece(pos)]
                    for k in range(len(masks)):
                        total = total + bufs[landing][k]
                    dst_ref[...] = total
            coefficient = bufs[plan[level][-1][6]][0].astype(BF16)
            if chunk == 0:
                loads[3 + 2 * level].wait()
            update(lo, level, coefficient)
        store = pltpu.make_async_copy(
            state.at[lo : lo + rows], out_hbm.at[lo : lo + rows], out_sems.at[chunk]
        )
        store.start()
        for copy in sends:
            copy.wait_send()
        yield
        store.wait()

    flows = [flow(chunk) for chunk in range(chunks)]
    while flows:
        left = []
        for item in flows:
            try:
                next(item)
                left.append(item)
            except StopIteration:
                pass
        flows = left


def shards(rhs, leaf_inverse, up_basis, projection):
    bits_x = lax.axis_size("gx").bit_length() - 1
    bits_y = lax.axis_size("gy").bit_length() - 1
    levels, rank, points = up_basis.shape
    rows = rhs.shape[0] // CHUNKS
    plan, shapes, sems = build_plan(levels, bits_x, rows, rank)
    dims = (bits_x, bits_y, levels, CHUNKS, rows, points, rank)
    any_spec = pl.BlockSpec(memory_space=pl.ANY)
    return pl.pallas_call(
        functools.partial(kernel, dims, plan),
        out_shape=jax.ShapeDtypeStruct(rhs.shape, F32),
        in_specs=[any_spec] * 4,
        out_specs=any_spec,
        scratch_shapes=[
            pltpu.VMEM(rhs.shape, BF16),
            pltpu.VMEM(leaf_inverse.shape[1:], BF16),
            pltpu.VMEM(up_basis.shape, BF16),
            pltpu.VMEM(projection.shape, BF16),
            pltpu.VMEM(rhs.shape, F32),
            pltpu.VMEM(rhs.shape, BF16),
            pltpu.SemaphoreType.DMA((2 + 2 * levels,)),
            pltpu.SemaphoreType.DMA((CHUNKS,)),
            pltpu.SemaphoreType.DMA((CHUNKS, sems)),
            pltpu.SemaphoreType.DMA((CHUNKS, sems)),
        ]
        + [pltpu.VMEM(shape, F32) for _ in range(CHUNKS) for shape in shapes],
        compiler_params=pltpu.CompilerParams(
            collective_id=0, has_side_effects=True, vmem_limit_bytes=60 * 2**20
        ),
    )(rhs, leaf_inverse, up_basis, projection)


def solution(mesh):
    return jax.shard_map(
        shards,
        mesh=mesh,
        in_specs=(
            P(None, ("gy", "gx")),
            P(("gy", "gx"), None, None),
            P(None, None, ("gy", "gx")),
            P(None, None, ("gy", "gx")),
        ),
        out_specs=P(None, ("gy", "gx")),
        check_vma=False,
    )
```

time: 183 us -> 82.5 us (0.45)
  waiting for transfers between devices: 137 us -> 0 us
  Pallas kernels: 0 us -> 79.2 us
  matrix products: 23.1 us -> 0 us
  starting transfers between devices: 14.8 us -> 0 us
  local copies, waits for them, and re-layouts: 5.61 us -> 3.16 us
  other arithmetic: 2.02 us -> 0 us
    ppermute x15 -> x0, waiting for transfers between devices: 137 us -> none  [partner(): return lax.ppermute(value, axis, pairs)]
    pallas_call x0 -> x1, Pallas kernels: none -> 79.2 us  [shards(): pl.pallas_call(functools.partial(kernel, dims, plan), out_shape=jax.Shape...]
    dot_general x11 -> x0, matrix products: 23.1 us -> none  [the longest x5 11.4 us: shards(): jnp.dot(coefficient, up_basis[height - 1], preferred_element_type=jnp.flo...]
    ppermute x15 -> x0, starting transfers between devices: 14.8 us -> none  [partner(): return lax.ppermute(value, axis, pairs)]
    unnamed x16 -> x1, local copies, waits for them, and re-layouts: 5.55 us -> 3.16 us
    add x10 -> x0, other arithmetic: 2.02 us -> none  [the longest x3 1.82 us: node_sum(): partial_value = partial_value + partner(partial_value, 'gx', bit_pos)]
  transfers between devices with their start and end apart: 15 -> 0, of which waited for: 15 -> 0; matrix products, arithmetic and copies ran while one was open for 0% -> 0% of each run, Pallas kernels for 0% -> 0%
where the time goes in v1:
time: 82.5 us; the launch traced here: 82.4 us
  Pallas kernels  79.2 us (96%)
  local copies, waits for them, and re-layouts  3.16 us (4%)
    pallas_call x1, Pallas kernels, shards(): pl.pallas_call(functools.partial(kernel, dims, plan), out_shape=jax.Shape...  79.2 us
    unnamed x1, local copies, waits for them, and re-layouts  3.16 us

profile of v1, /device:TPU:0, one launch (start us, length us, event | category | flops | bytes accessed | tf_op | source)
XLA Modules:
  0.0 82.4 jit_solution(8268546343802428259)
XLA Ops:
  0.0 79.2 %shard_map.46 = f32[512,1024]{1,0:T(8,128)} custom-call(bf16[512,1024]{1,0:T(8,128)(2,1)} %rhs_hbm.1, bf16[1,1024,1024]{2,1,0:T(8,128)(2,1)} %leaf_hbm.1, bf16[5,128,1024]{2,1,0:T(8,128)(2,1)} %up_hbm.1, bf16[5,256,1024]{2,1,0:T(8,128)(2,1)} %proj_hbm.1), custom_call_target="tpu_custom_call" | custom-call | tf_op jit(solution)/shard_map/pallas_call | solution.py:242
  79.2 3.2 %copy.6 = f32[512,1024]{1,0:T(8,128)} copy(f32[512,1024]{1,0:T(8,128)} %shard_map.46) | data formatting | bytes 4194304

commit v2 on v1

--- a/solution.py
+++ b/solution.py
@@ -9,7 +9,7 @@
 
 CHUNKS = 2
 SUBLANES = 8
-TILE = 256
+TILE = 1024
 F32 = jnp.float32
 BF16 = jnp.bfloat16
 
@@ -23,13 +23,16 @@
         groups.append([top])
     elif top > bits_x:
         groups.append([bits_x])
-        groups.append([top] + high[1:])
-    if top < bits_x and len(low) < 2:
+        last = [top] + high[1:]
+        if len(low) <= 3 and rows >> len(low) + len(high) >= SUBLANES:
+            last, low = last + low, []
+        groups.append(last)
+    if top < bits_x and len(low) < 3:
         groups.append(low + [top])
     else:
         while low:
-            groups.append(low[:2])
-            low = low[2:]
+            groups.append(low[:3])
+            low = low[3:]
         if top < bits_x:
             groups.append([top])
     phases = []
@@ -94,7 +97,7 @@
     return plan, shapes, sems
 
 
-def kernel(dims, plan, rhs_hbm, leaf_hbm, up_hbm, proj_hbm, out_hbm, *scratch):
+def kernel(dims, plan, rhs_hbm, leaf_hbm, up_hbm, proj_hbm, out_hbm, last_ref, *scratch):
     bits_x, bits_y, levels, chunks, rows, points, rank = dims
     rhs, leaf, up, proj, state, rounded = scratch[:6]
     in_sems, out_sems, send_sems, recv_sems = scratch[6:10]
@@ -111,7 +114,8 @@
     ]
     for level in range(levels):
         loads.append(pltpu.make_async_copy(proj_hbm.at[level], proj.at[level], in_sems.at[2 + 2 * level]))
-        loads.append(pltpu.make_async_copy(up_hbm.at[level], up.at[level], in_sems.at[3 + 2 * level]))
+        if level < levels - 1:
+            loads.append(pltpu.make_async_copy(up_hbm.at[level], up.at[level], in_sems.at[3 + 2 * level]))
     for load in loads:
         load.start()
 
@@ -207,13 +211,17 @@
                         total = total + bufs[landing][k]
                     dst_ref[...] = total
             coefficient = bufs[plan[level][-1][6]][0].astype(BF16)
+            if level == levels - 1:
+                last_ref[lo : lo + rows, :] = coefficient
+                break
             if chunk == 0:
                 loads[3 + 2 * level].wait()
             update(lo, level, coefficient)
-        store = pltpu.make_async_copy(
-            state.at[lo : lo + rows], out_hbm.at[lo : lo + rows], out_sems.at[chunk]
-        )
-        store.start()
+            if level == levels - 2:
+                store = pltpu.make_async_copy(
+                    state.at[lo : lo + rows], out_hbm.at[lo : lo + rows], out_sems.at[chunk]
+                )
+                store.start()
         for copy in sends:
             copy.wait_send()
         yield
@@ -239,11 +247,14 @@
     plan, shapes, sems = build_plan(levels, bits_x, rows, rank)
     dims = (bits_x, bits_y, levels, CHUNKS, rows, points, rank)
     any_spec = pl.BlockSpec(memory_space=pl.ANY)
-    return pl.pallas_call(
+    state, coefficient = pl.pallas_call(
         functools.partial(kernel, dims, plan),
-        out_shape=jax.ShapeDtypeStruct(rhs.shape, F32),
+        out_shape=(
+            jax.ShapeDtypeStruct(rhs.shape, F32),
+            jax.ShapeDtypeStruct((rhs.shape[0], rank), BF16),
+        ),
         in_specs=[any_spec] * 4,
-        out_specs=any_spec,
+        out_specs=(any_spec, pl.BlockSpec(memory_space=pltpu.VMEM)),
         scratch_shapes=[
             pltpu.VMEM(rhs.shape, BF16),
             pltpu.VMEM(leaf_inverse.shape[1:], BF16),
@@ -261,6 +272,7 @@
             collective_id=0, has_side_effects=True, vmem_limit_bytes=60 * 2**20
         ),
     )(rhs, leaf_inverse, up_basis, projection)
+    return state - jnp.dot(coefficient, up_basis[levels - 1], preferred_element_type=F32)
 
 
 def solution(mesh):

time: 82.5 us -> 73.3 us (0.89)
  Pallas kernels: 79.2 us -> 69.6 us
  matrix products: 0 us -> 3.51 us
  local copies, waits for them, and re-layouts: 3.16 us -> 0 us
    pallas_call x1, Pallas kernels: 79.2 us -> 69.6 us  [shards(): pl.pallas_call(functools.partial(kernel, dims, plan), out_shape=(jax.Shap...]
    dot_general x0 -> x1, matrix products: none -> 3.51 us  [shards(): jnp.dot(coefficient, up_basis[levels - 1], preferred_element_type=F32)]
    unnamed x1 -> x0, local copies, waits for them, and re-layouts: 3.16 us -> none
where the time goes in v2:
time: 73.3 us; the launch traced here: 73.1 us
  Pallas kernels  69.6 us (95%)
  matrix products  3.51 us (5%)
    pallas_call x1, Pallas kernels, shards(): pl.pallas_call(functools.partial(kernel, dims, plan), out_shape=(jax.Shap...  69.6 us
    dot_general x1, matrix products, shards(): jnp.dot(coefficient, up_basis[levels - 1], preferred_element_type=F32)  3.51 us

profile of v2, /device:TPU:0, one launch (start us, length us, event | category | flops | bytes accessed | tf_op | source)
XLA Modules:
  0.0 73.1 jit_solution(16269928456249662373)
XLA Ops:
  0.0 69.6 %shard_map.46 = (f32[512,1024]{1,0:T(8,128)}, bf16[512,128]{1,0:T(8,128)(2,1)}) custom-call(bf16[512,1024]{1,0:T(8,128)(2,1)} %rhs_hbm.1, bf16[1,1024,1024]{2,1,0:T(8,128)(2,1)} %leaf_hbm.1, bf16[5,128,1024]{2,1,0:T(8,128)(2,1)} %up_hbm.1, bf16[5,256,1024]{2,1,0:T(8,128)(2,1)} %proj_hbm.1), custom_call_target="tpu_custom_call" | custom-call | tf_op jit(solution)/shard_map/pallas_call | solution.py:250
  69.6 3.5 %convolution_subtract_fusion = f32[512,1024]{1,0:T(8,128)} fusion(f32[512,1024]{1,0:T(8,128)} %get-tuple-element.7, bf16[512,128]{1,0:T(8,128)(2,1)} %get-tuple-element.8, bf16[5,128,1024]{2,1,0:T(8,128)(2,1)} %up_hbm.1), kind=kOutput, calls=%fused_computation | convolution fusion | flops 134742016 | bytes 4587520 | tf_op jit(solution)/shard_map/dot_general | solution.py:275
